TPU v7x, 128 devices: a whole 4x4x4 slice. The times are simulated.
128 devices in a mesh: rows: 64 (over x, y, z_lo, core), res: 2 (over z_hi).
Axes of the slice: x: 4, y: 4, z: 4 (z_hi: 2, z_lo: 2; z = z_hi * 2 + z_lo), core: 2. Of those that a mesh axis runs over, the one named last changes fastest.
Arguments:
- base_runs: bfloat16 [262144, 32], P(('rows', 'res')), may hold values from -100 to 100
- other_runs: bfloat16 [262144, 32], P(('rows', 'res')), may hold values from -100 to 100
- mixed_runs: bfloat16 [262144, 4096], P(('rows', 'res')), may hold values from -100 to 100
- counts: int32 [256, 262144], P(None, ('rows', 'res')), may hold values from 0 to 4
Outputs:
- first_order: float32 [256, 4096], P('res', 'rows')
- total_order: float32 [256, 4096], P('res', 'rows')
All inputs are finite; a program needn't handle non-finite values.
Results may differ from a plain program's by a relative error of at most 0.0003.
Values sent between devices are 32-bit elements; how exact they have to be, the bound alone decides.
A program may use at most 192 MiB of HBM per device.

v0:
```python
import jax
import jax.numpy as jnp
from jax import lax
from jax.sharding import Mesh
from jax.sharding import PartitionSpec as P

ROWS_RES = ("rows_0", "rows_1", "rows_2", "rows_3", "res")
ROWS = ("rows_0", "rows_1", "rows_2", "rows_3")


def in_blocks(array, dim, count):
    lengths = array.shape
    blocks = array.reshape(*lengths[:dim], count, lengths[dim] // count, *lengths[dim + 1 :])
    return jnp.moveaxis(blocks, dim, 0)


def scatter_pairs(array, chips, core, dim):
    sizes = (lax.axis_size(chips), lax.axis_size(core))
    blocks = in_blocks(array, dim, sizes[0] * sizes[1])
    inside = blocks.shape[1:]
    blocks = blocks.reshape(*sizes, *inside).swapaxes(0, 1).reshape(-1, *inside)
    blocks = lax.psum_scatter(blocks, core, scatter_dimension=0, tiled=True)
    return lax.psum_scatter(blocks, chips, scatter_dimension=0, tiled=True)[0]


def summed_on_arrival(array, axis, dim):
    blocks = in_blocks(array, dim, lax.axis_size(axis))
    arrived = lax.all_to_all(blocks, axis, split_axis=0, concat_axis=0, tiled=True)
    return arrived.sum(axis=0)


def moment_inputs(base_runs, other_runs, mixed_runs):
    row_total = base_runs.shape[0]
    width = base_runs.shape[1]
    base_wide = base_runs.astype(jnp.float32)
    other_wide = other_runs.astype(jnp.float32)
    mixed_wide = mixed_runs.astype(jnp.float32).reshape(row_total, -1, width)
    change = mixed_wide - base_wide[:, None, :]
    cross = other_wide[:, None, :] * change
    square = change * change
    moment_terms = (
        jnp.concatenate([cross, square], axis=2).reshape(row_total, -1).astype(jnp.bfloat16)
    )
    moments = jnp.concatenate(
        [base_wide + other_wide, base_wide * base_wide + other_wide * other_wide], axis=1
    ).astype(jnp.bfloat16)
    return (moment_terms, moments)


def indices(weighted, base_sums, total_count, width):
    weight = jnp.maximum(total_count, 1.0)[:, None]
    mean_value = base_sums[:, :width] / (2.0 * weight)
    variance = jnp.maximum(base_sums[:, width:] / (2.0 * weight) - mean_value * mean_value, 0.25)
    shaped = weighted.reshape(weighted.shape[0], -1, 2 * width)
    scaled = (weight * variance)[:, None, :]
    first_order = (shaped[:, :, :width] / scaled).reshape(weighted.shape[0], -1)
    total_order = (shaped[:, :, width:] / (2.0 * scaled)).reshape(weighted.shape[0], -1)
    return (first_order, total_order)


def shards(base_runs, other_runs, mixed_runs, counts):
    width = base_runs.shape[1]
    resamples = counts.shape[0]
    moment_terms, moments = moment_inputs(base_runs, other_runs, mixed_runs)
    weights = counts.astype(jnp.bfloat16)
    base_part = jnp.dot(weights, moments, preferred_element_type=jnp.float32)
    count_part = jnp.sum(counts.astype(jnp.float32), axis=1)
    base_sums, total_count = lax.psum((base_part, count_part), ROWS_RES)
    groups = lax.axis_size("res")
    own_count = resamples // groups
    full_tile = jnp.dot(weights, moment_terms, preferred_element_type=jnp.float32)
    columns = scatter_pairs(full_tile, ("rows_0", "rows_1", "rows_2"), "rows_3", 1)
    owned_block = summed_on_arrival(columns, "res", 0)
    first_row = lax.axis_index("res") * own_count
    base_own = lax.dynamic_slice_in_dim(base_sums, first_row, own_count, 0)
    count_own = lax.dynamic_slice_in_dim(total_count, first_row, own_count, 0)
    first_order, total_order = indices(owned_block, base_own, count_own, width)
    return (first_order, total_order)


def solution(mesh):
    split = Mesh(
        mesh.devices.reshape(4, 4, 2, 2, mesh.shape["res"]),
        ("rows_0", "rows_1", "rows_2", "rows_3", "res"),
    )
    placed = (P(ROWS_RES, None), P(ROWS_RES, None), P(ROWS_RES, None), P(None, ROWS_RES))
    return jax.shard_map(
        shards,
        mesh=split,
        in_specs=placed,
        out_specs=(P("res", ROWS), P("res", ROWS)),
        check_vma=False,
    )
```

profile of v0, /device:TPU:0, one launch (start us, length us, event | category | flops | bytes accessed | tf_op | source)
XLA Modules:
  0.0 313.6 jit_solution(3321202897315099615)
XLA Ops:
  8.0 0.0 copy-start.1
  8.0 0.0 copy-start.2
  8.0 0.0 reduce-scatter.3.cloned.1.call-start
  8.1 22.6 %copy.19 = bf16[2048,4096]{0,1:T(8,128)(2,1)} copy(bf16[2048,4096]{1,0:T(8,128)(2,1)} %param.6) | data formatting | bytes 33554432 | tf_op args[2]
  30.7 0.0 copy-done.1
  30.7 0.0 copy-done.2
  30.8 19.6 %fusion.2 = (bf16[2048,128,32]{0,2,1:T(8,128)(2,1)}, bf16[2048,128,32]{0,2,1:T(8,128)(2,1)}) fusion(bf16[2048,128,32]{0,2,1:T(8,128)(2,1)} %bitcast.19, f32[2048,32]{0,1:T(8,128)S(1)} %convert_element_type.19, f32[2048,32]{0,1:T(8,128)S(1)} %convert_element_type.18), kind=kLoop, calls=%fused_computation.4 | loop fusion | flops 50331648 | bytes 50855936 | tf_op jit(solution)/shard_map/convert.3
  50.3 0.0 copy-start
  50.3 22.9 %pad_maximum_fusion = bf16[2048,128,64]{0,2,1:T(8,128)(2,1)} fusion(bf16[2048,128,32]{0,2,1:T(8,128)(2,1)} %get-tuple-element.7, bf16[2048,128,32]{0,2,1:T(8,128)(2,1)} %get-tuple-element.6), kind=kLoop, calls=%fused_computation | loop fusion | flops 67108864 | bytes 67108864 | tf_op jit(solution)/shard_map/concatenate | solution.py:42
  73.2 0.0 copy-done
  73.2 17.1 %fusion.5 = f32[8192,256]{1,0:T(8,128)} fusion(bf16[2048,8192]{0,1:T(8,128)(2,1)} %bitcast.20, s32[256,2048]{1,0:T(8,128)S(1)} %copy-done), kind=kOutput, calls=%fused_computation.9 | convolution fusion | flops 8590458880 | bytes 44040192 | tf_op jit(solution)/shard_map/dot_general | solution.py:71
  90.3 8.9 %copy.21 = f32[2,32,256,128]{3,2,1,0:T(8,128)} copy(f32[2,32,256,128]{2,3,0,1:T(8,128)} %bitcast.22) | data formatting | bytes 16777216 | tf_op jit(solution)/shard_map/transpose | solution.py:21
  99.2 0.0 reduce-scatter.3.cloned.1.call-update
  99.2 0.0 reduce-scatter.5.cloned.1.call-start
  99.3 21.7 %reduce-scatter.3.cloned.1.call-done = f32[32,256,128]{2,1,0:T(8,128)} async-done(((f32[64,256,128]{2,1,0:T(8,128)}), f32[32,256,128]{2,1,0:T(8,128)}) %reduce-scatter.3.cloned.1.call-update) | async-done | bytes 4194320 | tf_op jit(solution)/shard_map/reduce_scatter | solution.py:22
  121.0 0.0 reduce-scatter.5.cloned.1.call-update
  121.1 0.0 all-reduce.2.cloned.1.call-start
  121.1 0.1 add_convert_fusion.1
  121.2 1.1 convolution_bitcast_fusion
  122.3 0.0 all-reduce.2.cloned.1.call-update
  122.3 0.2 convert_reduce_fusion
  122.5 68.3 %psum.14 = f32[256]{0:T(256)S(1)} all-reduce(f32[256]{0:T(256)S(1)} %convert_reduce_fusion), channel_id=1, replica_groups=mesh['rows_0'=4,'rows_1'=4,'rows_2'=2,'rows_3'=2,'res'=2] {'rows_0','row..., use_global_device_ids=true, to_apply=%region_4.0 | all-reduce | flops 256 | bytes 2048 | tf_op jit(solution)/shard_map/psum | solution.py:68
  190.8 0.1 broadcast_multiply_fusion.1
  190.9 104.9 %reduce-scatter.5.cloned.1.call-done = f32[1,256,128]{2,1,0:T(8,128)} async-done(((f32[32,256,128]{2,1,0:T(8,128)}), f32[1,256,128]{2,1,0:T(8,128)}) %reduce-scatter.5.cloned.1.call-update) | async-done | bytes 131088 | tf_op jit(solution)/shard_map/reduce_scatter | solution.py:23
  295.8 3.7 %all-to-all-start = ((f32[2,128,128]{2,1,0:T(8,128)}), f32[2,128,128]{2,1,0:T(8,128)S(1)}, u32[]{:S(2)}, u32[]{:S(2)}) async-start(f32[2,128,128]{2,1,0:T(8,128)} %bitcast.24), calls=%async_computation.2 | async-start | bytes 262144 | tf_op jit(solution)/shard_map/all_to_all | solution.py:28
  299.5 0.0 all-reduce.2.cloned.1.call-done
  299.5 0.7 broadcast_multiply_fusion
  300.2 5.2 %all-to-all-done = f32[2,128,128]{2,1,0:T(8,128)S(1)} async-done(((f32[2,128,128]{2,1,0:T(8,128)}), f32[2,128,128]{2,1,0:T(8,128)S(1)}, u32[]{:S(2)}, u32[]{:S(2)}) %all-to-all-start) | async-done | bytes 131104 | tf_op jit(solution)/shard_map/all_to_all | solution.py:28
  305.5 0.1 copy.22
  305.6 0.6 slice_divide_fusion
  (3 shorter events, 0.0 us)
Async XLA Ops:
  8.0 22.7 %copy-start.1 = (bf16[2048,32]{0,1:T(8,128)(2,1)S(1)}, bf16[2048,32]{0,1:T(8,128)(2,1)}, u32[]{:S(2)}) copy-start(bf16[2048,32]{0,1:T(8,128)(2,1)} %param.4) | copy-start | bytes 393220
  8.0 22.7 %copy-start.2 = (bf16[2048,32]{0,1:T(8,128)(2,1)S(1)}, bf16[2048,32]{0,1:T(8,128)(2,1)}, u32[]{:S(2)}) copy-start(bf16[2048,32]{0,1:T(8,128)(2,1)} %param.5) | copy-start | bytes 393220
  8.0 113.0 %reduce-scatter.3.cloned.1.call-start = ((), (), s32[]{:S(2)}) async-start(), calls=%async_computation.3 | async-start | bytes 12582912 | tf_op jit(solution)/shard_map/reduce_scatter | solution.py:22
  50.3 22.9 %copy-start = (s32[256,2048]{1,0:T(8,128)S(1)}, s32[256,2048]{1,0:T(8,128)}, u32[]{:S(2)}) copy-start(s32[256,2048]{1,0:T(8,128)} %param.7) | copy-start | bytes 6291460
  99.2 196.6 %reduce-scatter.5.cloned.1.call-start = ((), (), s32[]{:S(2)}) async-start(), calls=%async_computation.4 | async-start | bytes 4325376 | tf_op jit(solution)/shard_map/reduce_scatter | solution.py:23
  121.1 178.4 %all-reduce.2.cloned.1.call-start = ((), (), s32[]{:S(2)}) async-start(), calls=%async_computation.5 | async-start | bytes 131072 | tf_op jit(solution)/shard_map/psum | solution.py:68
  295.8 9.6 %all-to-all-start = ((f32[2,128,128]{2,1,0:T(8,128)}), f32[2,128,128]{2,1,0:T(8,128)S(1)}, u32[]{:S(2)}, u32[]{:S(2)}) async-start(f32[2,128,128]{2,1,0:T(8,128)} %bitcast.24), calls=%async_computation.2 | async-start | bytes 262144 | tf_op jit(solution)/shard_map/all_to_all | solution.py:28
Sparse Core Ops, SparseCore 0:
  99.4 21.6 reduce-scatter.2
  123.4 172.3 reduce-scatter.4
Sparse Core Ops, SparseCore 1:
  126.3 143.7 all-reduce.1
where the time goes:
time: 315 us; the launch traced here: 314 us
  waiting for transfers between devices  132 us (42%)
  blocking collectives  68.3 us (22%)
  other arithmetic  44.3 us (14%)
  local copies, waits for them, and re-layouts  31.6 us (10%)
  matrix products  18.2 us (6%)
  between operations  15.6 us (5%)
  starting transfers between devices  3.79 us (1%)
    reduce_scatter x1, waiting for transfers between devices, scatter_pairs(): return lax.psum_scatter(blocks, chips, scatter_dimension=0, tiled=True)[0]  105 us
    psum x1, blocking collectives, shards(): base_sums, total_count = lax.psum((base_part, count_part), ROWS_RES)  68.3 us
    concatenate x1, other arithmetic, moment_inputs(): jnp.concatenate([cross, square], axis=2).reshape(row_total, -1)  22.9 us
    unnamed x7, local copies, waits for them, and re-layouts  22.6 us
    reduce_scatter x1, waiting for transfers between devices, scatter_pairs(): blocks = lax.psum_scatter(blocks, core, scatter_dimension=0, tiled=True)  21.7 us
    another operation x2, other arithmetic  19.6 us
    dot_general x1, matrix products, shards(): jnp.dot(weights, moment_terms, preferred_element_type=jnp.float32)  17.1 us
    transpose x1, local copies, waits for them, and re-layouts, scatter_pairs(): blocks = blocks.reshape(*sizes, *inside).swapaxes(0, 1).reshape(-1, *inside)  8.9 us
  transfers between devices with their start and end apart: 4, of which 3 were waited for; matrix products, arithmetic and copies ran while one was open for 1% of the time, Pallas kernels for 0%

commit v1 on v0

v1 whole, which is shorter than its diff:
```python
import jax
import jax.numpy as jnp
from jax import lax
from jax.experimental import pallas as pl
from jax.experimental.pallas import tpu as pltpu
from jax.sharding import Mesh
from jax.sharding import PartitionSpec as P

MESH = pl.DeviceIdType.MESH
AXES = ("x", "y", "zl", "core", "zh")

ORDER = (
    (2, 2), (2, 1), (1, 2), (2, 3), (3, 2), (1, 1), (1, 3), (3, 1),
    (3, 3), (2, 0), (0, 2), (1, 0), (0, 1), (3, 0), (0, 3), (0, 0),
)
STEPS = len(ORDER)
DX_CODE = sum(dx << (2 * i) for i, (dx, dy) in enumerate(ORDER))
DY_CODE = sum(dy << (2 * i) for i, (dx, dy) in enumerate(ORDER))
DX_LO, DX_HI = DX_CODE & 0xFFFF, DX_CODE >> 16
DY_LO, DY_HI = DY_CODE & 0xFFFF, DY_CODE >> 16
AHEAD = 6
LAG = 4
ROWS = (((0, 24), (24, 24)), ((48, 24), (72, 16)), ((88, 16), (104, 24)))


def digit(lo, hi, s):
    code = jnp.where(s < 8, lo, hi)
    return lax.shift_right_logical(code, 2 * (s % 8)) & 3


def coords(s):
    s = jnp.asarray(s, jnp.int32)
    return digit(DX_LO, DX_HI, s), digit(DY_LO, DY_HI, s)


def kernel(
    base_hbm, other_hbm, mixed_hbm, counts_hbm,
    first_ref, total_ref,
    base_v, other_v, counts_v, cbf, a4, b4, mbuf, terms0, terms1, stage, part,
    ra0, ra1, rb0, rb1, rc0, rc1,
    q0, q1, q2, q3, q4, q5,
    v0, v1, v2, v3, v4, v5,
    ustage, upart, uz, uy, ux, ufin,
    in_sem, msem, d2d_send, d2d_recv,
    recv1, recv_c, send1, recv2, recv3, send23, usend, urecv,
):
    x = lax.axis_index("x")
    y = lax.axis_index("y")
    zl = lax.axis_index("zl")
    core = lax.axis_index("core")
    zh = lax.axis_index("zh")
    z = zh * 2 + zl

    def at_x(d):
        return {"x": (x + d) % 4}

    def at_y(d):
        return {"y": (y + d) % 4}

    def at_z(d):
        target = (z + d) % 4
        return {"zl": target % 2, "zh": target // 2}

    partner = {"core": 1 - core}
    axes = (at_x, at_y, at_z)

    barrier = pltpu.get_barrier_semaphore()
    peers = [partner] + [ax(d) for ax in axes for d in (1, 2, 3)]
    for peer in peers:
        pl.semaphore_signal(barrier, inc=1, device_id=peer, device_id_type=MESH)

    def mixed_copy(t):
        s = t // 2
        dx, dy = coords(s)
        column = ((((x + dx) % 4) * 4 + (y + dy) % 4) * 2 + (zl + t) % 2) * 128
        return pltpu.make_async_copy(
            mixed_hbm.at[:, pl.ds(pl.multiple_of(column, 128), 128)], mbuf.at[t], msem.at[t]
        )

    counts_copy = pltpu.make_async_copy(counts_hbm, counts_v, in_sem.at[0])
    base_copy = pltpu.make_async_copy(base_hbm, base_v, in_sem.at[1])
    other_copy = pltpu.make_async_copy(other_hbm, other_v, in_sem.at[2])
    base_copy.start()
    other_copy.start()
    counts_copy.start()
    for t in range(AHEAD):
        mixed_copy(t).start()

    lane = lax.broadcasted_iota(jnp.int32, (32, 128), 1)
    row = lax.broadcasted_iota(jnp.int32, (32, 128), 0)
    repeat = (lane % 32 == row).astype(jnp.float32).astype(jnp.bfloat16)
    base_copy.wait()
    other_copy.wait()
    for r in range(0, 2048, 256):
        rs = pl.ds(r, 256)
        a4[rs, :] = jnp.dot(base_v[rs, :], repeat, preferred_element_type=jnp.float32)
        b4[rs, :] = jnp.dot(other_v[rs, :], repeat, preferred_element_type=jnp.float32)
    lane64 = lax.broadcasted_iota(jnp.int32, (64, 128), 1)
    for r in range(0, 2048, 64):
        rs = pl.ds(r, 64)
        av, bv = a4[rs, :], b4[rs, :]
        tail = jnp.where(lane64 == 64, 1.0, 0.0)
        value = jnp.where(lane64 < 32, av + bv, jnp.where(lane64 < 64, av * av + bv * bv, tail))
        terms1[rs, :128] = value.astype(jnp.bfloat16)
    counts_copy.wait()
    for r in range(0, 256, 8):
        rs = pl.ds(r, 8)
        cbf[rs, :] = counts_v[rs, :].astype(jnp.float32).astype(jnp.bfloat16)
    sums = jnp.dot(cbf[...], terms1[:, :128], preferred_element_type=jnp.float32)
    for q in range(2):
        for c in range(2):
            ustage[c, q] = sums[q * 128 + c * 64 : q * 128 + c * 64 + 64, :]

    def make_terms(t, out):
        for r in range(0, 2048, 64):
            rs = pl.ds(r, 64)
            change = mbuf[t, rs, :].astype(jnp.float32) - a4[rs, :]
            out[rs, :128] = (b4[rs, :] * change).astype(jnp.bfloat16)
            out[rs, 128:] = (change * change).astype(jnp.bfloat16)

    mixed_copy(0).wait()
    make_terms(0, terms0)

    pl.semaphore_wait(barrier, len(peers))

    def remote(src, dst, send, recv, target):
        return pltpu.make_async_remote_copy(
            src_ref=src, dst_ref=dst, send_sem=send, recv_sem=recv,
            device_id=target, device_id_type=MESH,
        )

    def u_d2d():
        return remote(ustage.at[1 - core], upart, usend.at[0], urecv.at[0], partner)

    def u_z(d):
        target_zh = ((z + d) % 4) // 2
        return remote(upart.at[target_zh], uz.at[d - 1], usend.at[d], urecv.at[d], at_z(d))

    def u_y(d):
        return remote(uz.at[3], uy.at[d - 1], usend.at[3 + d], urecv.at[3 + d], at_y(d))

    def u_x(d):
        return remote(uy.at[3], ux.at[d - 1], usend.at[6 + d], urecv.at[6 + d], at_x(d))

    def u_fin():
        return remote(ux.at[3], ufin.at[core], usend.at[10], urecv.at[10], partner)

    u_d2d().start()

    def u_stage1():
        u_d2d().wait_recv()
        for q in range(2):
            upart[q] = upart[q] + ustage[core, q]
        for d in (1, 2, 3):
            u_z(d).start()

    def u_stage2():
        for d in (1, 2, 3):
            u_z(d).wait_recv()
        uz[3] = upart[zh] + uz[0] + uz[1] + uz[2]
        for d in (1, 2, 3):
            u_y(d).start()

    def u_stage3():
        for d in (1, 2, 3):
            u_y(d).wait_recv()
        uy[3] = uz[3] + uy[0] + uy[1] + uy[2]
        for d in (1, 2, 3):
            u_x(d).start()

    def u_stage4():
        for d in (1, 2, 3):
            u_x(d).wait_recv()
        ux[3] = uy[3] + ux[0] + ux[1] + ux[2]
        u_fin().start()

    lane128 = lax.broadcasted_iota(jnp.int32, (128, 128), 1)

    def d2d(t):
        s = t // 2
        dx, dy = coords(s)
        return remote(
            stage.at[t, 1 - core], part.at[dx, dy, t % 2], d2d_send.at[t], d2d_recv.at[t], partner
        )

    def multiply(t, dzl, terms):
        result = jnp.dot(cbf[...], terms[...], preferred_element_type=jnp.float32)
        carry = (zl + dzl) // 2
        for q in range(2):
            cross = result[q * 128 : q * 128 + 128, :128]
            square = result[q * 128 : q * 128 + 128, 128:]
            j = (q + zh + carry) % 2
            stage[t, 0, j] = jnp.where(lane128 < 64, cross, pltpu.roll(square, 64, 1))
            stage[t, 1, j] = jnp.where(lane128 < 64, pltpu.roll(cross, 64, 1), square)
        d2d(t).start()

    def compute(s):
        t = 2 * s

        @pl.when(t + AHEAD < 2 * STEPS)
        def _():
            mixed_copy(t + AHEAD).start()
            mixed_copy(t + AHEAD + 1).start()

        mixed_copy(t + 1).wait()
        make_terms(t + 1, terms1)
        multiply(t, 0, terms0)

        @pl.when(t + 2 < 2 * STEPS)
        def _():
            mixed_copy(t + 2).wait()

        make_terms(jnp.minimum(t + 2, 2 * STEPS - 1), terms0)
        multiply(t + 1, 1, terms1)

    def rows(color, h):
        first, count = ROWS[color][h]
        return pl.ds(first, count)

    bufs1 = ((ra0, ra1), (rb0, rb1), (rc0, rc1))

    def message(color, h, dx, dy, direction):
        sem = recv1.at[color, h, dx * 4 + dy]
        return remote(
            part.at[dx, dy, :, :, rows(color, h), :], bufs1[color][h].at[dx, dy],
            send1.at[color, h], sem, axes[color](direction),
        )

    def message_z(h, dx, dy, dz, direction):
        return remote(
            part.at[dx, dy, dz % 2, dz // 2, rows(2, h), :], bufs1[2][h].at[dx, dy, dz - 1],
            send1.at[2, h], recv_c.at[h, dz - 1, dx * 4 + dy], at_z(direction),
        )

    def combine(s):
        dx, dy = coords(s)
        for dzl in range(2):
            t = 2 * s + dzl
            d2d(t).wait_recv()
            for j in range(2):
                part[dx, dy, dzl, j] = part[dx, dy, dzl, j] + stage[t, core, j]
        for color, d in ((0, dx), (1, dy)):

            @pl.when(d == 2)
            def _(color=color):
                message(color, 0, dx, dy, 1).start()
                message(color, 1, dx, dy, 3).start()

            @pl.when(d == 1)
            def _(color=color):
                message(color, 1, dx, dy, 1).start()

            @pl.when(d == 3)
            def _(color=color):
                message(color, 0, dx, dy, 3).start()

        message_z(0, dx, dy, 2, 1).start()
        message_z(1, dx, dy, 2, 3).start()
        message_z(1, dx, dy, 1, 1).start()
        message_z(0, dx, dy, 3, 3).start()

    def forward(s):
        dx, dy = coords(s)
        for color, d in ((0, dx), (1, dy)):
            from_dx, from_dy = (2, dy) if color == 0 else (dx, 2)

            @pl.when(d == 1)
            def _(color=color, from_dx=from_dx, from_dy=from_dy):
                message(color, 0, from_dx, from_dy, 1).wait_recv()
                view = part.at[dx, dy, :, :, rows(color, 0), :]
                view[...] = view[...] + bufs1[color][0][from_dx, from_dy]
                message(color, 0, dx, dy, 1).start()

            @pl.when(d == 3)
            def _(color=color, from_dx=from_dx, from_dy=from_dy):
                message(color, 1, from_dx, from_dy, 3).wait_recv()
                view = part.at[dx, dy, :, :, rows(color, 1), :]
                view[...] = view[...] + bufs1[color][1][from_dx, from_dy]
                message(color, 1, dx, dy, 3).start()

        for h, dz, direction in ((0, 1, 1), (1, 3, 3)):
            message_z(h, dx, dy, 2, direction).wait_recv()
            view = part.at[dx, dy, dz % 2, dz // 2, rows(2, h), :]
            view[...] = view[...] + bufs1[2][h][dx, dy, 1]
            message_z(h, dx, dy, dz, direction).start()

    @pl.loop(0, STEPS + LAG)
    def _(s):
        @pl.when(s < STEPS)
        def _():
            compute(s)

        @pl.when((s >= 1) & (s < STEPS + 1))
        def _():
            combine(s - 1)

        @pl.when(s >= LAG)
        def _():
            forward(s - LAG)

        for at, todo in ((1, u_stage1), (5, u_stage2), (9, u_stage3), (13, u_stage4)):
            @pl.when(s == at)
            def _(todo=todo):
                todo()

    bufs2 = ((q0, q1), (q2, q3), (q4, q5))
    bufs3 = ((v0, v1), (v2, v3), (v4, v5))

    def view2(color, h, d):
        if color == 0:
            return part.at[0, d, :, :, rows(0, h), :]
        if color == 1:
            return part.at[:, 0, d % 2, d // 2, rows(1, h), :]
        return part.at[d, :, 0, 0, rows(2, h), :]

    def finish1(color, h, d):
        buf = bufs1[color][h]
        view = view2(color, h, d)
        if color == 0:
            for side in (1, 3):
                message(0, h, side, d, 1).wait_recv()
            view[...] = view[...] + buf[1, d] + buf[3, d]
        elif color == 1:
            if d == 2:
                for dx in range(4):
                    for side in (1, 3):
                        message(1, h, dx, side, 1).wait_recv()
            view[...] = view[...] + buf[:, 1, d % 2, d // 2] + buf[:, 3, d % 2, d // 2]
        else:
            for dy in range(4):
                for dz in (1, 3):
                    message_z(h, d, dy, dz, 1).wait_recv()
            view[...] = view[...] + buf[d, :, 0] + buf[d, :, 2]

    axis2 = (at_y, at_z, at_x)
    axis3 = (at_z, at_x, at_y)

    def message2(color, h, d, direction):
        return remote(
            view2(color, h, d), bufs2[color][h].at[d - 1],
            send23.at[0, color, h, d - 1], recv2.at[color, h, d - 1], axis2[color](direction),
        )

    def view3(color, h, d):
        if color == 0:
            return part.at[0, 0, d % 2, d // 2, rows(0, h), :]
        if color == 1:
            return part.at[d, 0, 0, 0, rows(1, h), :]
        return part.at[0, d, 0, 0, rows(2, h), :]

    def message3(color, h, d, direction):
        return remote(
            view3(color, h, d), bufs3[color][h].at[d - 1],
            send23.at[1, color, h, d - 1], recv3.at[color, h, d - 1], axis3[color](direction),
        )

    def finish2(color, h, d):
        if d == 2:
            for side in (1, 3):
                message2(color, h, side, 1).wait_recv()
        buf = bufs2[color][h]
        view = view3(color, h, d)
        pick = (d % 2, d // 2) if color == 0 else (d,)
        view[...] = view[...] + buf[(0,) + pick] + buf[(2,) + pick]

    streams = [(color, h) for color in range(3) for h in range(2)]

    def phase(finish, message_of, view_of, bufs):
        for color, h in streams:
            finish(color, h, 2)
            message_of(color, h, 2, 1 if h == 0 else 3).start()
        for color, h in streams:
            d = 3 if h == 0 else 1
            finish(color, h, d)
            message_of(color, h, d, d).start()
        for color, h in streams:
            d = 1 if h == 0 else 3
            finish(color, h, d)
            message_of(color, h, 2, d).wait_recv()
            view = view_of(color, h, d)
            view[...] = view[...] + bufs[color][h][1]
            message_of(color, h, d, d).start()
        for color, h in streams:
            finish(color, h, 0)

    phase(finish1, message2, view2, bufs2)
    phase(finish2, message3, view3, bufs3)

    u_fin().wait_recv()
    ufin[core] = ux[3]
    rolled = []
    for c in range(2):
        sums_c = ufin[c]
        weight = jnp.maximum(sums_c[:, 64:65], 1.0)
        mean = sums_c / (2.0 * weight)
        square_mean = pltpu.roll(sums_c, 96, 1) / (2.0 * weight)
        variance = jnp.maximum(square_mean - mean * mean, 0.25)
        lanes = lax.broadcasted_iota(jnp.int32, (64, 128), 1)
        scaled = jnp.where(lanes < 32, weight * variance, 0.0)
        scaled = scaled + pltpu.roll(scaled, 32, 1)
        scaled = scaled + pltpu.roll(scaled, 64, 1)
        rolled.append(jnp.where(lanes < 64, scaled, 2.0 * scaled))
    divisor = jnp.concatenate(rolled, axis=0)

    for t in range(2 * STEPS):
        d2d(t).wait_send()
    for color in range(2):
        for h in range(2):
            sent = bufs1[color][h].at[:3]
            pltpu.make_async_copy(sent, sent, send1.at[color, h]).wait()
    for h in range(2):
        sent = bufs1[2][h]
        pltpu.make_async_copy(sent, sent, send1.at[2, h]).wait()
    u_d2d().wait_send()
    for d in (1, 2, 3):
        u_z(d).wait_send()
        u_y(d).wait_send()
        u_x(d).wait_send()
    u_fin().wait_send()
    for color, h in streams:
        for d in (1, 2, 3):
            message2(color, h, d, 1).wait_send()
            message3(color, h, d, 1).wait_send()

    for color, h in streams:
        for d in (1, 3):
            message3(color, h, d, 1).wait_recv()
        buf = bufs3[color][h]
        view = view3(color, h, 0)
        view[...] = view[...] + buf[0] + buf[2]

    result = part[0, 0, 0, 0] / divisor
    first_ref[...] = result[:, :64]
    total_ref[...] = pltpu.roll(result, 64, 1)[:, :64]


def shards(base_runs, other_runs, mixed_runs, counts):
    f32, bf16 = jnp.float32, jnp.bfloat16
    dma = pltpu.SemaphoreType.DMA

    def vmem(*shape, dtype=f32):
        return pltpu.VMEM(shape, dtype)

    sizes = [[count for first, count in color] for color in ROWS]
    scratch = [
        vmem(2048, 32, dtype=bf16), vmem(2048, 32, dtype=bf16), vmem(256, 2048, dtype=jnp.int32),
        vmem(256, 2048, dtype=bf16), vmem(2048, 128), vmem(2048, 128),
        vmem(32, 2048, 128, dtype=bf16), vmem(2048, 256, dtype=bf16), vmem(2048, 256, dtype=bf16),
        vmem(32, 2, 2, 128, 128), vmem(4, 4, 2, 2, 128, 128),
    ]
    for color in range(2):
        for h in range(2):
            scratch.append(vmem(4, 4, 2, 2, sizes[color][h], 128))
    for h in range(2):
        scratch.append(vmem(4, 4, 3, sizes[2][h], 128))
    for h in range(2):
        scratch.append(vmem(3, 2, 2, sizes[0][h], 128))
    for color in (1, 2):
        for h in range(2):
            scratch.append(vmem(3, 4, sizes[color][h], 128))
    for color in range(3):
        for h in range(2):
            scratch.append(vmem(3, sizes[color][h], 128))
    scratch += [
        vmem(2, 2, 64, 128), vmem(2, 64, 128), vmem(4, 64, 128), vmem(4, 64, 128),
        vmem(4, 64, 128), vmem(2, 64, 128),
        dma((3,)), dma((32,)), dma((32,)), dma((32,)),
        dma((2, 2, 16)), dma((2, 3, 16)), dma((3, 2)), dma((3, 2, 3)), dma((3, 2, 3)),
        dma((2, 3, 2, 3)), dma((11,)), dma((11,)),
    ]
    any_spec = pl.BlockSpec(memory_space=pl.ANY)
    out = jax.ShapeDtypeStruct((128, 64), f32)
    return pl.pallas_call(
        kernel,
        out_shape=(out, out),
        in_specs=[any_spec] * 4,
        out_specs=(pl.BlockSpec(memory_space=pltpu.VMEM),) * 2,
        scratch_shapes=scratch,
        compiler_params=pltpu.CompilerParams(
            collective_id=0, has_side_effects=True, vmem_limit_bytes=64 * 1024 * 1024 - 65536
        ),
    )(base_runs, other_runs, mixed_runs, counts)


def solution(mesh):
    split = Mesh(mesh.devices.reshape(4, 4, 2, 2, mesh.shape["res"]), AXES)
    every = AXES
    columns = ("x", "y", "zl", "core")
    placed = (P(every, None), P(every, None), P(every, None), P(None, every))
    return jax.shard_map(
        shards,
        mesh=split,
        in_specs=placed,
        out_specs=(P("zh", columns), P("zh", columns)),
        check_vma=False,
    )
```

time: 315 us -> 72.7 us (0.23)
  waiting for transfers between devices: 132 us -> 0 us
  blocking collectives: 68.3 us -> 0 us
  Pallas kernels: 0 us -> 64.9 us
  other arithmetic: 44.3 us -> 0 us
  local copies, waits for them, and re-layouts: 31.6 us -> 6.89 us
  matrix products: 18.2 us -> 0 us
  between operations: 15.6 us -> 0.64 us
  starting transfers between devices: 3.79 us -> 0 us
    reduce_scatter x2 -> x0, waiting for transfers between devices: 127 us -> none  [the longest x1 105 us: scatter_pairs(): return lax.psum_scatter(blocks, chips, scatter_dimension=0, tiled=True)[0]]
    psum x1 -> x0, blocking collectives: 68.3 us -> none  [shards(): base_sums, total_count = lax.psum((base_part, count_part), ROWS_RES)]
    pallas_call x0 -> x1, Pallas kernels: none -> 64.9 us  [shards(): pl.pallas_call(kernel, out_shape=(out, out), in_specs=[any_spec] * 4, out...]
    concatenate x1 -> x0, other arithmetic: 22.9 us -> none  [moment_inputs(): jnp.concatenate([cross, square], axis=2).reshape(row_total, -1)]
    another operation x2 -> x0, other arithmetic: 19.6 us -> none
    unnamed x7 -> x2, local copies, waits for them, and re-layouts: 22.6 us -> 3.82 us
    dot_general x2 -> x0, matrix products: 18.2 us -> none  [the longest x1 17.1 us: shards(): jnp.dot(weights, moment_terms, preferred_element_type=jnp.float32)]
    transpose x1 -> x0, local copies, waits for them, and re-layouts: 8.9 us -> none  [scatter_pairs(): blocks = blocks.reshape(*sizes, *inside).swapaxes(0, 1).reshape(-1, *inside)]
  transfers between devices with their start and end apart: 4 -> 0, of which waited for: 3 -> 0; matrix products, arithmetic and copies ran while one was open for 1% -> 0% of each run, Pallas kernels for 0% -> 0%
where the time goes in v1:
time: 72.7 us; the launch traced here: 72.4 us
  Pallas kernels  64.9 us (89%)
  local copies, waits for them, and re-layouts  6.89 us (9%)
    pallas_call x1, Pallas kernels, shards(): pl.pallas_call(kernel, out_shape=(out, out), in_specs=[any_spec] * 4, out...  64.9 us
    unnamed x2, local copies, waits for them, and re-layouts  3.82 us
    pallas_call x2, local copies, waits for them, and re-layouts, shards(): pl.pallas_call(kernel, out_shape=(out, out), in_specs=[any_spec] * 4, out...  3.07 us

profile of v1, /device:TPU:0, one launch (start us, length us, event | category | flops | bytes accessed | tf_op | source)
XLA Modules:
  0.0 72.4 jit_solution(2807905801652278629)
XLA Ops:
  0.6 1.9 %copy.6.base_hbm = bf16[2048,32]{1,0:T(8,128)(2,1)} copy(bf16[2048,32]{0,1:T(8,128)(2,1)} %param.4) | data formatting | bytes 262144 | tf_op args[0]
  2.5 1.9 %copy.7.other_hbm = bf16[2048,32]{1,0:T(8,128)(2,1)} copy(bf16[2048,32]{0,1:T(8,128)(2,1)} %param.5) | data formatting | bytes 262144 | tf_op args[1]
  4.5 64.9 %shard_map.59 = (f32[128,64]{1,0:T(8,128)}, f32[128,64]{1,0:T(8,128)}) custom-call(bf16[2048,32]{1,0:T(8,128)(2,1)} %copy.6.base_hbm, bf16[2048,32]{1,0:T(8,128)(2,1)} %copy.7.other_hbm, bf16[2048,4096]{1,0:T(8,128)(2,1)} %mixed_hbm.1, s32[256,2048]{1,0:T(8,128)} %counts_hbm.1), custom_call_target="tpu_custom_call" | custom-call | tf_op jit(solution)/shard_map/pallas_call | solution.py:473
  69.4 1.5 %copy.8 = f32[128,64]{0,1:T(8,128)} copy(f32[128,64]{1,0:T(8,128)} %get-tuple-element.2) | data formatting | bytes 65536 | tf_op jit(solution)/shard_map/pallas_call | solution.py:473
  70.9 1.5 %copy.9 = f32[128,64]{0,1:T(8,128)} copy(f32[128,64]{1,0:T(8,128)} %get-tuple-element.3) | data formatting | bytes 65536 | tf_op jit(solution)/shard_map/pallas_call | solution.py:473

commit v2 on v1

v2 whole, which is shorter than its diff:
```python
import functools

import jax
import jax.numpy as jnp
from jax import lax
from jax.experimental import pallas as pl
from jax.experimental.pallas import tpu as pltpu
from jax.sharding import Mesh
from jax.sharding import PartitionSpec as P

MESH = pl.DeviceIdType.MESH
AXES = ("x", "y", "zl", "core", "zh")

ORDER = (
    (2, 2), (2, 1), (1, 2), (2, 3), (3, 2), (1, 1), (1, 3), (3, 1),
    (3, 3), (2, 0), (0, 2), (1, 0), (0, 1), (3, 0), (0, 3), (0, 0),
)
STEPS = len(ORDER)
DX_CODE = sum(dx << (2 * i) for i, (dx, dy) in enumerate(ORDER))
DY_CODE = sum(dy << (2 * i) for i, (dx, dy) in enumerate(ORDER))
DX_LO, DX_HI = DX_CODE & 0xFFFF, DX_CODE >> 16
DY_LO, DY_HI = DY_CODE & 0xFFFF, DY_CODE >> 16
AHEAD = 6
DEPTH = 256
ENTER = 2
COMBINE = 2
ARRIVE = 6
ROWS = (((0, 24), (24, 24)), ((48, 24), (72, 16)), ((88, 16), (104, 24)))


def digit(lo, hi, s):
    code = jnp.where(s < 8, lo, hi)
    return lax.shift_right_logical(code, 2 * (s % 8)) & 3


def coords(s):
    s = jnp.asarray(s, jnp.int32)
    return digit(DX_LO, DX_HI, s), digit(DY_LO, DY_HI, s)


def order_of_work():
    A, B, C = range(3)
    work = []

    def add(time, name, *args):
        work.append((time, len(work), name, args))
        return time

    at = {pair: i for i, pair in enumerate(ORDER)}
    R = ARRIVE
    k, fab, fc = {}, {}, {}
    for pair, i in at.items():
        add(max(i, ENTER), "exchange", i)
        k[pair] = add(max(i, ENTER) + COMBINE, "combine", i)
    for (dx, dy), t in k.items():
        ready = [t]
        if dx in (1, 3):
            ready.append(k[2, dy] + R)
        if dy in (1, 3):
            ready.append(k[dx, 2] + R)
        fab[dx, dy] = max(ready)
        if dx in (1, 3):
            add(fab[dx, dy], "forward", A, 1, dx, (dy,))
        if dy in (1, 3):
            add(fab[dx, dy], "forward", B, 1, dy, (dx,))
        fc[dx, dy] = t + R
        for dz in (1, 3):
            add(fc[dx, dy], "forward", C, 1, dz, (dx, dy))
    a2 = {d: max(k[0, d], fab[1, d] + R, fab[3, d] + R) for d in range(4)}
    b2 = {d: max(k[d, 0], fab[d, 1] + R, fab[d, 3] + R) for d in range(4)}
    c2 = {pair: t + R for pair, t in fc.items()}
    for d in range(4):
        add(a2[d], "arrive", A, 1, (d,))
        if d:
            add(a2[d], "direct", A, 2, d, ())
        add(b2[d], "arrive", B, 1, (d,))
        for dz in (2, 1, 3):
            add(b2[d], "direct", B, 2, dz, (d,))
        for o in range(4):
            add(c2[d, o], "arrive", C, 1, (d, o))
            if d:
                add(c2[d, o], "direct", C, 2, d, (o,))
    a3 = max(a2[0], a2[1] + R, a2[2] + R, a2[3] + R)
    add(a3, "gather", A, 2, ())
    for dz in (2, 1, 3):
        add(a3, "direct", A, 3, dz, ())
    last = [add(a3 + R, "gather", A, 3, ())]
    b3 = {d: b2[d] + R for d in range(4)}
    c3 = {d: max(c2[0, d], *(c2[o, d] + R for o in (1, 2, 3))) for d in range(4)}
    for color, third in ((B, b3), (C, c3)):
        for d in range(4):
            add(third[d], "gather", color, 2, (d,))
            if d:
                add(third[d], "direct", color, 3, d, ())
        last.append(add(max(third[0], *(third[d] + R for d in (1, 2, 3))), "gather", color, 3, ()))
    work.sort()
    return work, last


def kernel(
    base_hbm, other_hbm, mixed_hbm, counts_hbm,
    first_ref, total_ref,
    base_v, other_v, counts_v, cbf, a4, b4, mbuf, stage, part,
    ra0, ra1, rb0, rb1, rc0, rc1,
    qa, qb, qc, va, vb, vc,
    ustage, upart, uz, uy, ux, ufin,
    in_sem, msem, d2d_send, d2d_recv,
    recv1, recv_c, recv2, recv3, send, usend, urecv,
):
    x = lax.axis_index("x")
    y = lax.axis_index("y")
    zl = lax.axis_index("zl")
    core = lax.axis_index("core")
    zh = lax.axis_index("zh")
    z = zh * 2 + zl

    def at_x(d):
        return {"x": (x + d) % 4}

    def at_y(d):
        return {"y": (y + d) % 4}

    def at_z(d):
        target = (z + d) % 4
        return {"zl": target % 2, "zh": target // 2}

    partner = {"core": 1 - core}
    axes = (at_x, at_y, at_z)

    barrier = pltpu.get_barrier_semaphore()
    peers = [partner] + [ax(d) for ax in axes for d in (1, 2, 3)]
    for peer in peers:
        pl.semaphore_signal(barrier, inc=1, device_id=peer, device_id_type=MESH)

    def mixed_copy(t):
        s = t // 2
        dx, dy = coords(s)
        column = ((((x + dx) % 4) * 4 + (y + dy) % 4) * 2 + (zl + t) % 2) * 128
        return pltpu.make_async_copy(
            mixed_hbm.at[:, pl.ds(pl.multiple_of(column, 128), 128)], mbuf.at[t], msem.at[t]
        )

    counts_copy = pltpu.make_async_copy(counts_hbm, counts_v, in_sem.at[0])
    base_copy = pltpu.make_async_copy(base_hbm, base_v, in_sem.at[1])
    other_copy = pltpu.make_async_copy(other_hbm, other_v, in_sem.at[2])
    base_copy.start()
    other_copy.start()
    counts_copy.start()
    for t in range(AHEAD):
        mixed_copy(t).start()

    lane = lax.broadcasted_iota(jnp.int32, (32, 128), 1)
    row = lax.broadcasted_iota(jnp.int32, (32, 128), 0)
    repeat = (lane % 32 == row).astype(jnp.float32).astype(jnp.bfloat16)
    base_copy.wait()
    other_copy.wait()
    for r in range(0, 2048, 256):
        rs = pl.ds(r, 256)
        for wide, runs in ((a4, base_v), (b4, other_v)):
            wide[rs, :] = lax.dot_general(
                runs[:, rs], repeat, (((0,), (0,)), ((), ())), preferred_element_type=jnp.float32
            )
    counts_copy.wait()
    for r in range(0, 256, 16):
        rs = pl.ds(r, 16)
        cbf[rs, :] = counts_v[rs, :].astype(jnp.float32).astype(jnp.bfloat16)

    lane256 = lax.broadcasted_iota(jnp.int32, (DEPTH, 128), 1)

    def moments_of(rs):
        av, bv = a4[rs, :], b4[rs, :]
        tail = jnp.where(lane256 == 64, 1.0, 0.0)
        value = jnp.where(lane256 < 32, av + bv, jnp.where(lane256 < 64, av * av + bv * bv, tail))
        return value.astype(jnp.bfloat16)

    def terms_of(t, rs):
        change = mbuf[t, rs, :].astype(jnp.float32) - a4[rs, :]
        cross = (b4[rs, :] * change).astype(jnp.bfloat16)
        square = (change * change).astype(jnp.bfloat16)
        return jnp.concatenate([cross, square], axis=1)

    def resampled(make):
        total = None
        for r in range(0, 2048, DEPTH):
            piece = jnp.dot(
                cbf[:, r : r + DEPTH], make(pl.ds(r, DEPTH)), preferred_element_type=jnp.float32
            )
            total = piece if total is None else total + piece
        return total

    sums = resampled(moments_of)
    for q in range(2):
        for c in range(2):
            ustage[c, q] = sums[q * 128 + c * 64 : q * 128 + c * 64 + 64, :]


    def remote(src, dst, send, recv, target):
        return pltpu.make_async_remote_copy(
            src_ref=src, dst_ref=dst, send_sem=send, recv_sem=recv,
            device_id=target, device_id_type=MESH,
        )

    def u_d2d():
        return remote(ustage.at[1 - core], upart, usend.at[0], urecv.at[0], partner)

    def u_z(d):
        target_zh = ((z + d) % 4) // 2
        return remote(upart.at[target_zh], uz.at[d - 1], usend.at[d], urecv.at[d], at_z(d))

    def u_y(d):
        return remote(uz.at[3], uy.at[d - 1], usend.at[3 + d], urecv.at[3 + d], at_y(d))

    def u_x(d):
        return remote(uy.at[3], ux.at[d - 1], usend.at[6 + d], urecv.at[6 + d], at_x(d))

    def u_fin():
        return remote(ux.at[3], ufin.at[core], usend.at[10], urecv.at[10], partner)


    def u_stage1():
        u_d2d().wait_recv()
        for q in range(2):
            upart[q] = upart[q] + ustage[core, q]
        for d in (1, 2, 3):
            u_z(d).start()

    def u_stage2():
        for d in (1, 2, 3):
            u_z(d).wait_recv()
        uz[3] = upart[zh] + uz[0] + uz[1] + uz[2]
        for d in (1, 2, 3):
            u_y(d).start()

    def u_stage3():
        for d in (1, 2, 3):
            u_y(d).wait_recv()
        uy[3] = uz[3] + uy[0] + uy[1] + uy[2]
        for d in (1, 2, 3):
            u_x(d).start()

    def u_stage4():
        for d in (1, 2, 3):
            u_x(d).wait_recv()
        ux[3] = uy[3] + ux[0] + ux[1] + ux[2]
        u_fin().start()

    lane128 = lax.broadcasted_iota(jnp.int32, (128, 128), 1)

    def d2d(t):
        dx, dy = ORDER[t // 2]
        return remote(
            stage.at[t, 1 - core], part.at[dx, dy, t % 2], d2d_send, d2d_recv.at[t], partner
        )

    def multiply(t, dzl):
        result = resampled(lambda rs: terms_of(t, rs))
        carry = (zl + dzl) // 2
        for q in range(2):
            cross = result[q * 128 : q * 128 + 128, :128]
            square = result[q * 128 : q * 128 + 128, 128:]
            j = (q + zh + carry) % 2
            stage[t, 0, j] = jnp.where(lane128 < 64, cross, pltpu.roll(square, 64, 1))
            stage[t, 1, j] = jnp.where(lane128 < 64, pltpu.roll(cross, 64, 1), square)

    def compute(s):
        t = 2 * s

        @pl.when(t + AHEAD < 2 * STEPS)
        def _():
            mixed_copy(t + AHEAD).start()
            mixed_copy(t + AHEAD + 1).start()

        mixed_copy(t).wait()
        mixed_copy(t + 1).wait()
        multiply(t, 0)
        multiply(t + 1, 1)

    bufs = {
        1: ((ra0, ra1), (rb0, rb1), (rc0, rc1)),
        2: ((qa,), (qb,), (qc,)),
        3: ((va,), (vb,), (vc,)),
    }

    def view(color, phase, d, other, h):
        if phase == 1:
            where = ((d, *other), (*other, d), (*other, d % 2, d // 2))[color]
        elif phase == 2:
            where = ((0, d), (*other, 0, d % 2, d // 2), (d, *other, 0, 0))[color]
        else:
            where = ((0, 0, d % 2, d // 2), (d, 0, 0, 0), (0, d, 0, 0))[color]
        first, count = ROWS[color][0] if phase > 1 else ROWS[color][h]
        if phase > 1:
            count += ROWS[color][1][1]
        full = (slice(None),) * (4 - len(where))
        return part.at[(*where, *full, pl.ds(first, count))]

    def message(color, phase, d, other, h, direction):
        flat = sum(o * 4**i for i, o in enumerate(other))
        if phase == 1:
            sem = recv_c.at[h, d - 1, flat] if color == 2 else recv1.at[color, h, d - 1, flat]
        elif phase == 2:
            sem = recv2.at[color, d - 1, flat]
        else:
            sem = recv3.at[color, d - 1]
        return remote(
            view(color, phase, d, other, h), bufs[phase][color][h].at[(d - 1, *other)],
            send.at[phase - 1, color, h], sem, axes[(color + phase - 1) % 3](direction),
        )

    def launch(color, phase, d, other):
        if d != 3:
            h = 1 if d == 1 else 0
            message(color, phase, d, other, h, 1).start()
        if d != 1:
            h = 0 if d == 3 else 1
            message(color, phase, d, other, h, 3).start()

    def forward(color, phase, d, other):
        h = 0 if d == 1 else 1
        message(color, phase, 2, other, h, d).wait_recv()
        here = view(color, phase, d, other, h)
        here[...] = here[...] + bufs[phase][color][h][(1, *other)]
        message(color, phase, d, other, h, d).start()

    def arrive(color, phase, other):
        for h in range(2):
            for d in (1, 3):
                message(color, phase, d, other, h, d).wait_recv()
            buf = bufs[phase][color][h]
            here = view(color, phase, 0, other, h)
            here[...] = here[...] + buf[(0, *other)] + buf[(2, *other)]

    def direct(color, phase, d, other):
        message(color, phase, d, other, 0, d).start()

    def gather(color, phase, other):
        for d in (1, 2, 3):
            message(color, phase, d, other, 0, d).wait_recv()
        buf = bufs[phase][color][0]
        here = view(color, phase, 0, other, 0)
        here[...] = (here[...] + buf[(0, *other)]) + (buf[(1, *other)] + buf[(2, *other)])

    def exchange(i):
        d2d(2 * i).start()
        d2d(2 * i + 1).start()

    def combine(i):
        dx, dy = ORDER[i]
        for dzl in range(2):
            d2d(2 * i + dzl).wait_recv()
            for j in range(2):
                part[dx, dy, dzl, j] = part[dx, dy, dzl, j] + stage[2 * i + dzl, core, j]
        if dx:
            launch(0, 1, dx, (dy,))
        if dy:
            launch(1, 1, dy, (dx,))
        for dz in (2, 1, 3):
            launch(2, 1, dz, (dx, dy))

    def enter():
        pl.semaphore_wait(barrier, len(peers))
        u_d2d().start()

    work, last = order_of_work()
    does = dict(exchange=exchange, combine=combine, launch=launch, forward=forward, arrive=arrive, direct=direct, gather=gather)
    todo = [(time, count, functools.partial(does[name], *args)) for time, count, name, args in work]
    todo.append((ENTER, -1, enter))
    for i, u_stage in enumerate((u_stage1, u_stage2, u_stage3, u_stage4)):
        todo.append((ENTER + 2 + 5 * i, -1, u_stage))
    todo.sort(key=lambda item: item[:2])
    final = [item for item in todo if item[0] >= min(last)]
    todo = todo[: len(todo) - len(final)]

    @pl.loop(0, STEPS)
    def _(s):
        compute(s)
        for quarter in range(0, STEPS, 4):

            @pl.when(s // 4 == quarter // 4)
            def _(quarter=quarter):
                for step in range(quarter, quarter + 4):
                    now = [run for time, count, run in todo if step - 1 < time <= step]
                    if now:

                        @pl.when(s == step)
                        def _(now=now):
                            for run in now:
                                run()

    for time, count, run in todo:
        if time > STEPS - 1:
            run()

    u_fin().wait_recv()
    ufin[core] = ux[3]
    rolled = []
    for c in range(2):
        sums_c = ufin[c]
        weight = jnp.maximum(sums_c[:, 64:65], 1.0)
        mean = sums_c / (2.0 * weight)
        square_mean = pltpu.roll(sums_c, 96, 1) / (2.0 * weight)
        variance = jnp.maximum(square_mean - mean * mean, 0.25)
        lanes = lax.broadcasted_iota(jnp.int32, (64, 128), 1)
        scaled = jnp.where(lanes < 32, weight * variance, 0.0)
        scaled = scaled + pltpu.roll(scaled, 32, 1)
        scaled = scaled + pltpu.roll(scaled, 64, 1)
        rolled.append(jnp.where(lanes < 64, scaled, 2.0 * scaled))
    divisor = jnp.concatenate(rolled, axis=0)

    def all_left(ref, sem):
        pltpu.make_async_copy(ref, ref, sem).wait()

    all_left(stage.at[:, 0], d2d_send)
    u_d2d().wait_send()
    for d in (1, 2, 3):
        u_z(d).wait_send()
        u_y(d).wait_send()
        u_x(d).wait_send()
    u_fin().wait_send()

    for time, count, run in final:
        run()
    for phase, colors in bufs.items():
        for color in range(3):
            for h, buf in enumerate(colors[color]):
                all_left(buf, send.at[phase - 1, color, h])

    result = part[0, 0, 0, 0] / divisor
    result = result.T
    first_ref[...] = result[:64]
    total_ref[...] = result[64:]


def shards(base_runs, other_runs, mixed_runs, counts):
    f32, bf16 = jnp.float32, jnp.bfloat16
    dma = pltpu.SemaphoreType.DMA

    def vmem(*shape, dtype=f32):
        return pltpu.VMEM(shape, dtype)

    sizes = [[count for first, count in color] for color in ROWS]
    scratch = [
        vmem(32, 2048, dtype=bf16), vmem(32, 2048, dtype=bf16), vmem(256, 2048, dtype=jnp.int32),
        vmem(256, 2048, dtype=bf16), vmem(2048, 128), vmem(2048, 128),
        vmem(32, 2048, 128, dtype=bf16),
        vmem(32, 2, 2, 128, 128), vmem(4, 4, 2, 2, 128, 128),
    ]
    inside = (
        ((3, 4, 2, 2), (3, 4, 2, 2), (3, 4, 4)),
        ((3, 2, 2), (3, 4), (3, 4)),
        ((3,), (3,), (3,)),
    )
    for phase, shapes in enumerate(inside, 1):
        for color in range(3):
            for count in sizes[color] if phase == 1 else [sum(sizes[color])]:
                scratch.append(vmem(*shapes[color], count, 128))
    scratch += [
        vmem(2, 2, 64, 128), vmem(2, 64, 128), vmem(4, 64, 128), vmem(4, 64, 128),
        vmem(4, 64, 128), vmem(2, 64, 128),
        dma((3,)), dma((32,)), dma, dma((32,)),
        dma((2, 2, 3, 4)), dma((2, 3, 16)), dma((3, 3, 4)), dma((3, 3)), dma((3, 3, 2)),
        dma((11,)), dma((11,)),
    ]
    any_spec = pl.BlockSpec(memory_space=pl.ANY)
    out = jax.ShapeDtypeStruct((64, 128), f32)
    first_order, total_order = pl.pallas_call(
        kernel,
        out_shape=(out, out),
        in_specs=[any_spec] * 4,
        out_specs=(pl.BlockSpec(memory_space=pltpu.VMEM),) * 2,
        scratch_shapes=scratch,
        compiler_params=pltpu.CompilerParams(
            collective_id=0, has_side_effects=True, vmem_limit_bytes=64 * 1024 * 1024 - 65536
        ),
    )(base_runs.T, other_runs.T, mixed_runs, counts)
    return first_order.T, total_order.T


def solution(mesh):
    split = Mesh(mesh.devices.reshape(4, 4, 2, 2, mesh.shape["res"]), AXES)
    every = AXES
    columns = ("x", "y", "zl", "core")
    placed = (P(every, None), P(every, None), P(every, None), P(None, every))
    return jax.shard_map(
        shards,
        mesh=split,
        in_specs=placed,
        out_specs=(P("zh", columns), P("zh", columns)),
        check_vma=False,
    )
```

time: 72.7 us -> 44.1 us (0.61)
  Pallas kernels: 64.9 us -> 40.5 us
  local copies, waits for them, and re-layouts: 6.89 us -> 2.75 us
    pallas_call x1, Pallas kernels: 64.9 us -> 40.5 us  [shards(): pl.pallas_call(kernel, out_shape=(out, out), in_specs=[any_spec] * 4, out...]
    pallas_call x2 -> x0, local copies, waits for them, and re-layouts: 3.07 us -> none  [shards(): pl.pallas_call(kernel, out_shape=(out, out), in_specs=[any_spec] * 4, out...]
    unnamed x2, local copies, waits for them, and re-layouts: 3.82 us -> 2.75 us
where the time goes in v2:
time: 44.1 us; the launch traced here: 43.8 us
  Pallas kernels  40.5 us (92%)
  local copies, waits for them, and re-layouts  2.75 us (6%)
  between operations  0.64 us (1%)
    pallas_call x1, Pallas kernels, shards(): pl.pallas_call(kernel, out_shape=(out, out), in_specs=[any_spec] * 4, out...  40.5 us
    unnamed x2, local copies, waits for them, and re-layouts  2.75 us

profile of v2, /device:TPU:0, one launch (start us, length us, event | category | flops | bytes accessed | tf_op | source)
XLA Modules:
  0.0 43.8 jit_solution(15642147334851774467)
XLA Ops:
  0.6 40.5 %shard_map.59 = (f32[64,128]{1,0:T(8,128)}, f32[64,128]{1,0:T(8,128)}) custom-call(bf16[32,2048]{1,0:T(8,128)(2,1)} %bitcast.4, bf16[32,2048]{1,0:T(8,128)(2,1)} %bitcast.5, bf16[2048,4096]{1,0:T(8,128)(2,1)} %mixed_hbm.1, s32[256,2048]{1,0:T(8,128)} %counts_hbm.1), custom_call_target="tpu_custom_call" | custom-call | tf_op jit(solution)/shard_map/pallas_call | solution.py:466
  41.1 1.4 %copy.8 = f32[128,64]{0,1:T(8,128)} copy(f32[128,64]{0,1:T(8,128)} %bitcast.7) | data formatting | bytes 65536
  42.5 1.4 %copy.9 = f32[128,64]{0,1:T(8,128)} copy(f32[128,64]{0,1:T(8,128)} %bitcast.6) | data formatting | bytes 65536

commit v3 on v2

--- a/solution.py
+++ b/solution.py
@@ -25,6 +25,7 @@
 ENTER = 2
 COMBINE = 2
 ARRIVE = 6
+DIRECT = (2,)
 ROWS = (((0, 24), (24, 24)), ((48, 24), (72, 16)), ((88, 16), (104, 24)))
 
 
@@ -53,31 +54,28 @@
         add(max(i, ENTER), "exchange", i)
         k[pair] = add(max(i, ENTER) + COMBINE, "combine", i)
     for (dx, dy), t in k.items():
-        ready = [t]
-        if dx in (1, 3):
-            ready.append(k[2, dy] + R)
-        if dy in (1, 3):
-            ready.append(k[dx, 2] + R)
-        fab[dx, dy] = max(ready)
-        if dx in (1, 3):
-            add(fab[dx, dy], "forward", A, 1, dx, (dy,))
-        if dy in (1, 3):
-            add(fab[dx, dy], "forward", B, 1, dy, (dx,))
-        fc[dx, dy] = t + R
-        for dz in (1, 3):
-            add(fc[dx, dy], "forward", C, 1, dz, (dx, dy))
-    a2 = {d: max(k[0, d], fab[1, d] + R, fab[3, d] + R) for d in range(4)}
-    b2 = {d: max(k[d, 0], fab[d, 1] + R, fab[d, 3] + R) for d in range(4)}
+        for color, d, other, across in ((A, dx, dy, (2, dy)), (B, dy, dx, (dx, 2))):
+            fab[color, dx, dy] = t
+            if d in (1, 3) and color not in DIRECT:
+                fab[color, dx, dy] = add(max(t, k[across] + R), "forward", color, 1, d, (other,))
+        fc[dx, dy] = t
+        if C not in DIRECT:
+            fc[dx, dy] = t + R
+            for dz in (1, 3):
+                add(fc[dx, dy], "forward", C, 1, dz, (dx, dy))
+    a2 = {d: max(k[0, d], *(fab[A, o, d] + R for o in (1, 2, 3))) for d in range(4)}
+    b2 = {d: max(k[d, 0], *(fab[B, d, o] + R for o in (1, 2, 3))) for d in range(4)}
+    reach = {color: "gather" if color in DIRECT else "arrive" for color in range(3)}
     c2 = {pair: t + R for pair, t in fc.items()}
     for d in range(4):
-        add(a2[d], "arrive", A, 1, (d,))
+        add(a2[d], reach[A], A, 1, (d,))
         if d:
             add(a2[d], "direct", A, 2, d, ())
-        add(b2[d], "arrive", B, 1, (d,))
+        add(b2[d], reach[B], B, 1, (d,))
         for dz in (2, 1, 3):
             add(b2[d], "direct", B, 2, dz, (d,))
         for o in range(4):
-            add(c2[d, o], "arrive", C, 1, (d, o))
+            add(c2[d, o], reach[C], C, 1, (d, o))
             if d:
                 add(c2[d, o], "direct", C, 2, d, (o,))
     a3 = max(a2[0], a2[1] + R, a2[2] + R, a2[3] + R)
@@ -99,10 +97,8 @@
 
 def kernel(
     base_hbm, other_hbm, mixed_hbm, counts_hbm,
-    first_ref, total_ref,
-    base_v, other_v, counts_v, cbf, a4, b4, mbuf, stage, part,
-    ra0, ra1, rb0, rb1, rc0, rc1,
-    qa, qb, qc, va, vb, vc,
+    sums_ref, divisor_ref,
+    base_v, other_v, counts_v, cbf, a4, b4, mbuf, stage, part, bufs,
     ustage, upart, uz, uy, ux, ufin,
     in_sem, msem, d2d_send, d2d_recv,
     recv1, recv_c, recv2, recv3, send, usend, urecv,
@@ -275,12 +271,6 @@
         multiply(t, 0)
         multiply(t + 1, 1)
 
-    bufs = {
-        1: ((ra0, ra1), (rb0, rb1), (rc0, rc1)),
-        2: ((qa,), (qb,), (qc,)),
-        3: ((va,), (vb,), (vc,)),
-    }
-
     def view(color, phase, d, other, h):
         if phase == 1:
             where = ((d, *other), (*other, d), (*other, d % 2, d // 2))[color]
@@ -288,8 +278,8 @@
             where = ((0, d), (*other, 0, d % 2, d // 2), (d, *other, 0, 0))[color]
         else:
             where = ((0, 0, d % 2, d // 2), (d, 0, 0, 0), (0, d, 0, 0))[color]
-        first, count = ROWS[color][0] if phase > 1 else ROWS[color][h]
-        if phase > 1:
+        first, count = ROWS[color][h]
+        if len(bufs[phase][color]) == 1:
             count += ROWS[color][1][1]
         full = (slice(None),) * (4 - len(where))
         return part.at[(*where, *full, pl.ds(first, count))]
@@ -331,14 +321,15 @@
             here[...] = here[...] + buf[(0, *other)] + buf[(2, *other)]
 
     def direct(color, phase, d, other):
-        message(color, phase, d, other, 0, d).start()
+        for h in range(len(bufs[phase][color])):
+            message(color, phase, d, other, h, d).start()
 
     def gather(color, phase, other):
-        for d in (1, 2, 3):
-            message(color, phase, d, other, 0, d).wait_recv()
-        buf = bufs[phase][color][0]
-        here = view(color, phase, 0, other, 0)
-        here[...] = (here[...] + buf[(0, *other)]) + (buf[(1, *other)] + buf[(2, *other)])
+        for h, buf in enumerate(bufs[phase][color]):
+            for d in (1, 2, 3):
+                message(color, phase, d, other, h, d).wait_recv()
+            here = view(color, phase, 0, other, h)
+            here[...] = (here[...] + buf[(0, *other)]) + (buf[(1, *other)] + buf[(2, *other)])
 
     def exchange(i):
         d2d(2 * i).start()
@@ -350,12 +341,13 @@
             d2d(2 * i + dzl).wait_recv()
             for j in range(2):
                 part[dx, dy, dzl, j] = part[dx, dy, dzl, j] + stage[2 * i + dzl, core, j]
+        leave = [direct if color in DIRECT else launch for color in range(3)]
         if dx:
-            launch(0, 1, dx, (dy,))
+            leave[0](0, 1, dx, (dy,))
         if dy:
-            launch(1, 1, dy, (dx,))
+            leave[1](1, 1, dy, (dx,))
         for dz in (2, 1, 3):
-            launch(2, 1, dz, (dx, dy))
+            leave[2](2, 1, dz, (dx, dy))
 
     def enter():
         pl.semaphore_wait(barrier, len(peers))
@@ -425,10 +417,8 @@
             for h, buf in enumerate(colors[color]):
                 all_left(buf, send.at[phase - 1, color, h])
 
-    result = part[0, 0, 0, 0] / divisor
-    result = result.T
-    first_ref[...] = result[:64]
-    total_ref[...] = result[64:]
+    sums_ref[...] = part[0, 0, 0, 0].T
+    divisor_ref[...] = divisor.T
 
 
 def shards(base_runs, other_runs, mixed_runs, counts):
@@ -450,10 +440,16 @@
         ((3, 2, 2), (3, 4), (3, 4)),
         ((3,), (3,), (3,)),
     )
-    for phase, shapes in enumerate(inside, 1):
-        for color in range(3):
-            for count in sizes[color] if phase == 1 else [sum(sizes[color])]:
-                scratch.append(vmem(*shapes[color], count, 128))
+    scratch.append({
+        phase: [
+            [
+                vmem(*shapes[color], count, 128)
+                for count in ([sum(sizes[color])] if phase > 1 or color in DIRECT else sizes[color])
+            ]
+            for color in range(3)
+        ]
+        for phase, shapes in enumerate(inside, 1)
+    })
     scratch += [
         vmem(2, 2, 64, 128), vmem(2, 64, 128), vmem(4, 64, 128), vmem(4, 64, 128),
         vmem(4, 64, 128), vmem(2, 64, 128),
@@ -462,8 +458,8 @@
         dma((11,)), dma((11,)),
     ]
     any_spec = pl.BlockSpec(memory_space=pl.ANY)
-    out = jax.ShapeDtypeStruct((64, 128), f32)
-    first_order, total_order = pl.pallas_call(
+    out = jax.ShapeDtypeStruct((128, 128), f32)
+    sums, divisor = pl.pallas_call(
         kernel,
         out_shape=(out, out),
         in_specs=[any_spec] * 4,
@@ -473,7 +469,7 @@
             collective_id=0, has_side_effects=True, vmem_limit_bytes=64 * 1024 * 1024 - 65536
         ),
     )(base_runs.T, other_runs.T, mixed_runs, counts)
-    return first_order.T, total_order.T
+    return (sums[:64] / divisor[:64]).T, (sums[64:] / divisor[64:]).T
 
 
 def solution(mesh):

time: 44.1 us -> 42.6 us (0.966)
  local copies, waits for them, and re-layouts: 2.75 us -> 0 us
  other arithmetic: 0 us -> 1.45 us
    unnamed x2 -> x0, local copies, waits for them, and re-layouts: 2.75 us -> none
    transpose x0 -> x1, other arithmetic: none -> 1.45 us  [shards(): return ((sums[:64] / divisor[:64]).T, (sums[64:] / divisor[64:]).T)]
where the time goes in v3:
time: 42.6 us; the launch traced here: 42.4 us
  Pallas kernels  40.4 us (95%)
  other arithmetic  1.45 us (3%)
  between operations  0.64 us (2%)
    pallas_call x1, Pallas kernels, shards(): pl.pallas_call(kernel, out_shape=(out, out), in_specs=[any_spec] * 4, out...  40.4 us
    transpose x1, other arithmetic, shards(): return ((sums[:64] / divisor[:64]).T, (sums[64:] / divisor[64:]).T)  1.45 us

profile of v3, /device:TPU:0, one launch (start us, length us, event | category | flops | bytes accessed | tf_op | source)
XLA Modules:
  0.0 42.4 jit_solution(3863504966364843028)
XLA Ops:
  0.6 40.4 %shard_map.59 = (f32[128,128]{1,0:T(8,128)}, f32[128,128]{1,0:T(8,128)}) custom-call(bf16[32,2048]{1,0:T(8,128)(2,1)} %bitcast.6, bf16[32,2048]{1,0:T(8,128)(2,1)} %bitcast.7, bf16[2048,4096]{1,0:T(8,128)(2,1)} %mixed_hbm.1, s32[256,2048]{1,0:T(8,128)} %counts_hbm.1), custom_call_target="tpu_custom_call" | custom-call | tf_op jit(solution)/shard_map/pallas_call | solution.py:462
  41.0 1.4 %divide_bitcast_fusion = (f32[128,64]{0,1:T(8,128)}, f32[128,64]{0,1:T(8,128)}) fusion(f32[128,128]{1,0:T(8,128)} %get-tuple-element.5, f32[128,128]{1,0:T(8,128)} %get-tuple-element.4), kind=kLoop, calls=%fused_computation | loop fusion | flops 16384 | bytes 196608 | tf_op jit(solution)/shard_map/transpose | solution.py:472

commit v4 on v3

--- a/solution.py
+++ b/solution.py
@@ -410,15 +410,15 @@
         u_x(d).wait_send()
     u_fin().wait_send()
 
-    for time, count, run in final:
-        run()
     for phase, colors in bufs.items():
+        if phase == 3:
+            divisor_ref[...] = divisor.T
+            for time, count, run in final:
+                run()
+            sums_ref[...] = part[0, 0, 0, 0].T
         for color in range(3):
             for h, buf in enumerate(colors[color]):
                 all_left(buf, send.at[phase - 1, color, h])
-
-    sums_ref[...] = part[0, 0, 0, 0].T
-    divisor_ref[...] = divisor.T
 
 
 def shards(base_runs, other_runs, mixed_runs, counts):

time: 42.6 us -> 42.6 us (level)
  no operation moved by 1% of the time
where the time goes in v4:
time: 42.6 us; the launch traced here: 42.4 us
  Pallas kernels  40.3 us (95%)
  other arithmetic  1.45 us (3%)
  between operations  0.64 us (2%)
    pallas_call x1, Pallas kernels, shards(): pl.pallas_call(kernel, out_shape=(out, out), in_specs=[any_spec] * 4, out...  40.3 us
    transpose x1, other arithmetic, shards(): return ((sums[:64] / divisor[:64]).T, (sums[64:] / divisor[64:]).T)  1.45 us

profile of v4, /device:TPU:0, one launch (start us, length us, event | category | flops | bytes accessed | tf_op | source)
XLA Modules:
  0.0 42.4 jit_solution(2051539460001837170)
XLA Ops:
  0.6 40.3 %shard_map.59 = (f32[128,128]{1,0:T(8,128)}, f32[128,128]{1,0:T(8,128)}) custom-call(bf16[32,2048]{1,0:T(8,128)(2,1)} %bitcast.6, bf16[32,2048]{1,0:T(8,128)(2,1)} %bitcast.7, bf16[2048,4096]{1,0:T(8,128)(2,1)} %mixed_hbm.1, s32[256,2048]{1,0:T(8,128)} %counts_hbm.1), custom_call_target="tpu_custom_call" | custom-call | tf_op jit(solution)/shard_map/pallas_call | solution.py:462
  41.0 1.4 %divide_bitcast_fusion = (f32[128,64]{0,1:T(8,128)}, f32[128,64]{0,1:T(8,128)}) fusion(f32[128,128]{1,0:T(8,128)} %get-tuple-element.5, f32[128,128]{1,0:T(8,128)} %get-tuple-element.4), kind=kLoop, calls=%fused_computation | loop fusion | flops 16384 | bytes 196608 | tf_op jit(solution)/shard_map/transpose | solution.py:472
